TPU v7x, 32 devices: a whole 2x2x4 slice. The times are simulated.
32 devices in a mesh: fsdp: 8 (over z, x), grp: 4 (over y, core).
Axes of the slice: x: 2, y: 2, z: 4, core: 2. Of those that a mesh axis runs over, the one named last changes fastest.
Arguments:
- gradient: bfloat16 [24, 512, 512], P('fsdp', 'grp'), may hold values from -6 to 6
- left_factor: bfloat16 [96, 512, 512], P(('fsdp', 'grp'))
- right_factor: bfloat16 [96, 512, 512], P(('fsdp', 'grp'))
- block_owner: int32 [24], replicated, may hold values from 0 to 31, as said below
Outputs:
- preconditioned: bfloat16 [24, 512, 512], P('fsdp', 'grp')
Inputs may be any that keep to these rules, and one draw needn't show every extreme that they name: block_owner[b] is a device index, fsdp index times 4 plus grp index. The 3 blocks homed at one fsdp index go to devices of 3 different fsdp indices; the devices of each fsdp index own 3 blocks in all; no device owns more than 3 blocks, and at every fsdp index one device owns exactly 3.
All inputs are finite; a program needn't handle non-finite values.
Results may differ from a plain program's by a relative error of at most 0.0049.
Values may be sent and summed in bfloat16 or wider, within the bound.
A program may use at most 64 MiB of HBM per device.

v0:
```python
import jax
import jax.numpy as jnp
from jax import lax
from jax.sharding import PartitionSpec as P


def per_device(gradient, left_factor, right_factor, block_owner):
    local_blocks = gradient.shape[0]
    piece_rows = gradient.shape[1]
    block_width = gradient.shape[2]
    slot_count = left_factor.shape[0]
    columns = lax.axis_size("fsdp")
    groups = lax.axis_size("grp")
    column = lax.axis_index("fsdp")
    owners_all = block_owner.reshape(columns, local_blocks)
    dest_column = owners_all // groups
    dest_group = owners_all % groups
    mine_column = lax.dynamic_index_in_dim(dest_column, column, 0, keepdims=False)
    column_ids = jnp.arange(columns, dtype=jnp.int32)
    matching = mine_column[None, :] == column_ids[:, None]
    pick_send = matching.astype(jnp.bfloat16)
    outgoing = jnp.einsum(
        "cj,jrd->crd", pick_send, gradient, preferred_element_type=jnp.float32
    ).astype(jnp.bfloat16)
    arrived = lax.all_to_all(
        outgoing.reshape(columns * piece_rows, block_width),
        "fsdp",
        split_axis=0,
        concat_axis=0,
        tiled=True,
    )
    arrived = arrived.reshape(columns, piece_rows, block_width)
    toward = dest_column == column
    live_source = jnp.sum(toward.astype(jnp.int32), axis=1) > 0
    target = jnp.sum(jnp.where(toward, dest_group, 0), axis=1)
    same_owner = (target[None, :] == target[:, None]) & live_source[None, :] & live_source[:, None]
    before = column_ids[None, :] < column_ids[:, None]
    rank_slot = jnp.sum((same_owner & before).astype(jnp.int32), axis=1)
    group_ids = jnp.arange(groups, dtype=jnp.int32)
    slot_ids = jnp.arange(slot_count, dtype=jnp.int32)
    routing = (
        live_source[None, None, :]
        & (target[None, None, :] == group_ids[:, None, None])
        & (rank_slot[None, None, :] == slot_ids[None, :, None])
    )
    routing = routing.astype(jnp.bfloat16)
    packed = jnp.einsum(
        "oks,srd->kord", routing, arrived, preferred_element_type=jnp.float32
    ).astype(jnp.bfloat16)
    packed = packed.reshape(slot_count, groups * piece_rows, block_width)
    blocks = lax.all_to_all(packed, "grp", split_axis=1, concat_axis=1, tiled=True)
    left_product = jnp.einsum(
        "kab,kbc->kac", left_factor, blocks, preferred_element_type=jnp.float32
    ).astype(jnp.bfloat16)
    result = jnp.einsum(
        "kab,kbc->kac", left_product, right_factor, preferred_element_type=jnp.float32
    ).astype(jnp.bfloat16)
    returned = lax.all_to_all(result, "grp", split_axis=1, concat_axis=1, tiled=True)
    returned = returned.reshape(slot_count, groups, piece_rows, block_width)
    unpacked = jnp.einsum(
        "oks,kord->srd", routing, returned, preferred_element_type=jnp.float32
    ).astype(jnp.bfloat16)
    homeward = lax.all_to_all(
        unpacked.reshape(columns * piece_rows, block_width),
        "fsdp",
        split_axis=0,
        concat_axis=0,
        tiled=True,
    )
    homeward = homeward.reshape(columns, piece_rows, block_width)
    return jnp.einsum(
        "cj,crd->jrd", pick_send, homeward, preferred_element_type=jnp.float32
    ).astype(jnp.bfloat16)


def solution(mesh):
    return jax.shard_map(
        per_device,
        mesh=mesh,
        in_specs=(
            P("fsdp", "grp", None),
            P(("fsdp", "grp"), None, None),
            P(("fsdp", "grp"), None, None),
            P(),
        ),
        out_specs=P("fsdp", "grp", None),
        check_vma=False,
    )
```

profile of v0, /device:TPU:0, one launch (start us, length us, event | category | flops | bytes accessed | tf_op | source)
XLA Modules:
  0.0 135.2 jit_solution(5954696607277778726)
XLA Ops:
  0.0 0.0 copy-start
  0.0 0.8 reshape.94
  0.9 1.6 %convolution_convert_fusion.3 = bf16[8,128,512]{2,0,1:T(8,128)(2,1)S(1)} fusion(bf16[3,128,512]{2,1,0:T(8,128)(2,1)} %param.4, s32[3]{0:T(128)S(1)} %dynamic-slice_bitcast_fusion), kind=kOutput, calls=%fused_computation.7 | convolution fusion | flops 3670040 | bytes 1441804 | tf_op jit(solution)/shard_map/cj,jrd->crd/dot_general | solution.py:22
  2.5 1.3 copy.33
  3.8 7.3 %all-to-all-start = ((bf16[8,128,512]{2,1,0:T(8,128)(2,1)}), bf16[8,128,512]{2,1,0:T(8,128)(2,1)S(1)}, u32[]{:S(2)}, u32[]{:S(2)}) async-start(bf16[8,128,512]{2,1,0:T(8,128)(2,1)} %copy.33), calls=%async_computation | async-start | bytes 2097152 | tf_op jit(solution)/shard_map/all_to_all | solution.py:25
  11.1 0.1 convert_reduce_fusion.1
  11.2 0.2 convert_reduce_fusion
  11.4 25.4 %all-to-all-done = bf16[8,128,512]{2,1,0:T(8,128)(2,1)S(1)} async-done(((bf16[8,128,512]{2,1,0:T(8,128)(2,1)}), bf16[8,128,512]{2,1,0:T(8,128)(2,1)S(1)}, u32[]{:S(2)}, u32[]{:S(2)}) %all-to-all-start) | async-done | bytes 1048608 | tf_op jit(solution)/shard_map/all_to_all | solution.py:25
  36.8 1.0 fusion.2
  37.9 0.3 copy.35
  38.2 1.4 copy.36
  39.6 28.9 %all_to_all.22 = bf16[3,512,512]{2,0,1:T(4,128)(2,1)} all-to-all(bf16[3,512,512]{2,0,1:T(4,128)(2,1)S(1)} %copy.36), channel_id=1, replica_groups=mesh['fsdp'=8,'grp'=4] {'grp'}, dimensions={1} | all-to-all | bytes 3145728 | tf_op jit(solution)/shard_map/all_to_all | solution.py:51
  68.5 0.0 copy-done
  68.5 4.2 %convolution_convert_fusion = bf16[3,512,512]{2,1,0:T(8,128)(2,1)S(1)} fusion(bf16[3,512,512]{2,1,0:T(8,128)(2,1)S(1)} %copy-done, bf16[3,512,512]{2,1,0:T(8,128)(2,1)} %param.5, bf16[3,512,512]{2,0,1:T(4,128)(2,1)} %all_to_all.22), kind=kOutput, calls=%fused_computation.1 | convolution fusion | flops 1612185600 | bytes 6291456 | tf_op jit(solution)/shard_map/kab,kbc->kac/dot_general | solution.py:55
  72.7 1.4 copy.39
  74.0 28.1 %all_to_all.23 = bf16[3,512,512]{2,0,1:T(4,128)(2,1)S(1)} all-to-all(bf16[3,512,512]{2,0,1:T(4,128)(2,1)S(1)} %copy.39), channel_id=1, replica_groups=mesh['fsdp'=8,'grp'=4] {'grp'}, dimensions={1} | all-to-all | bytes 3145728 | tf_op jit(solution)/shard_map/all_to_all | solution.py:58
  102.2 2.2 %bitcast_convert_fusion = bf16[8,128,512]{2,0,1:T(8,128)(2,1)S(1)} fusion(bf16[3,4,128,512]{3,0,2,1:T(4,128)(2,1)S(1)} %bitcast.23, pred[3,8]{1,0:T(4,128)(4,1)S(1)} %iota_compare_fusion.1, pred[4,8]{1,0:T(4,128)(4,1)S(1)} %fusion.22), kind=kOutput, calls=%fused_computation | convolution fusion | flops 13107296 | bytes 2621496 | tf_op jit(solution)/shard_map/oks,kord->srd/dot_general | solution.py:60
  104.4 0.3 copy.42
  104.7 28.8 %all_to_all.24 = bf16[8,128,512]{2,1,0:T(8,128)(2,1)S(1)} all-to-all(bf16[8,128,512]{2,1,0:T(8,128)(2,1)S(1)} %copy.42), channel_id=1, replica_groups=mesh['fsdp'=8,'grp'=4] {'fsdp'}, dimensions={0} | all-to-all | bytes 2097152 | tf_op jit(solution)/shard_map/all_to_all | solution.py:63
  133.6 0.8 convolution_convert_fusion.4
  134.4 0.8 copy.44
  (5 shorter events, 0.0 us)
Async XLA Ops:
  0.0 68.5 %copy-start = (bf16[3,512,512]{2,1,0:T(8,128)(2,1)S(1)}, bf16[3,512,512]{2,1,0:T(8,128)(2,1)}, u32[]{:S(2)}) copy-start(bf16[3,512,512]{2,1,0:T(8,128)(2,1)} %param.6) | copy-start | bytes 4718596
  3.8 33.0 %all-to-all-start = ((bf16[8,128,512]{2,1,0:T(8,128)(2,1)}), bf16[8,128,512]{2,1,0:T(8,128)(2,1)S(1)}, u32[]{:S(2)}, u32[]{:S(2)}) async-start(bf16[8,128,512]{2,1,0:T(8,128)(2,1)} %copy.33), calls=%async_computation | async-start | bytes 2097152 | tf_op jit(solution)/shard_map/all_to_all | solution.py:25
where the time goes:
time: 136 us; the launch traced here: 135 us
  blocking collectives  85.9 us (63%)
  waiting for transfers between devices  25.4 us (19%)
  matrix products  9.85 us (7%)
  starting transfers between devices  7.28 us (5%)
  local copies, waits for them, and re-layouts  6.34 us (5%)
    all_to_all x1, blocking collectives, per_device(): lax.all_to_all(packed, 'grp', split_axis=1, concat_axis=1, tiled=True)  28.9 us
    all_to_all x1, blocking collectives, per_device(): lax.all_to_all(unpacked.reshape(columns * piece_rows, block_width), 'fsdp...  28.8 us
    all_to_all x1, blocking collectives, per_device(): lax.all_to_all(result, 'grp', split_axis=1, concat_axis=1, tiled=True)  28.1 us
    all_to_all x1, waiting for transfers between devices, per_device(): lax.all_to_all(outgoing.reshape(columns * piece_rows, block_width), 'fsdp...  25.4 us
    all_to_all x1, starting transfers between devices, per_device(): lax.all_to_all(outgoing.reshape(columns * piece_rows, block_width), 'fsdp...  7.28 us
    dot_general x1, matrix products, per_device(): jnp.einsum('kab,kbc->kac', left_product, right_factor, preferred_element_...  4.21 us
  transfers between devices with their start and end apart: 1, of which 1 were waited for; matrix products, arithmetic and copies ran while one was open for 0% of the time, Pallas kernels for 0%

commit v1 on v0

--- a/solution.py
+++ b/solution.py
@@ -48,7 +48,20 @@
         "oks,srd->kord", routing, arrived, preferred_element_type=jnp.float32
     ).astype(jnp.bfloat16)
     packed = packed.reshape(slot_count, groups * piece_rows, block_width)
-    blocks = lax.all_to_all(packed, "grp", split_axis=1, concat_axis=1, tiled=True)
+
+    def turns_attach(w_in, device_axis):
+        x_new = jnp.concatenate(
+            lax.all_to_all(
+                jnp.stack(jnp.split(w_in, lax.psum(1, device_axis), axis=1), axis=0),
+                device_axis,
+                0,
+                0,
+            ),
+            axis=1,
+        )
+        return x_new
+
+    blocks = turns_attach(packed, "grp")
     left_product = jnp.einsum(
         "kab,kbc->kac", left_factor, blocks, preferred_element_type=jnp.float32
     ).astype(jnp.bfloat16)

time: 136 us -> 129 us (0.949)
  blocking collectives: 85.9 us -> 79.6 us
    all_to_all x1, blocking collectives: 28.9 us -> 22.6 us  [turns_attach(): lax.all_to_all(jnp.stack(jnp.split(w_in, lax.psum(1, device_axis), axis=1...]
where the time goes in v1:
time: 129 us
  blocking collectives  79.6 us (62%)
  waiting for transfers between devices  25.4 us (20%)
  matrix products  9.51 us (7%)
  starting transfers between devices  7.28 us (6%)
  local copies, waits for them, and re-layouts  6.35 us (5%)
    all_to_all x1, blocking collectives, per_device(): lax.all_to_all(unpacked.reshape(columns * piece_rows, block_width), 'fsdp...  28.8 us
    all_to_all x1, blocking collectives, per_device(): lax.all_to_all(result, 'grp', split_axis=1, concat_axis=1, tiled=True)  28.1 us
    all_to_all x1, waiting for transfers between devices, per_device(): lax.all_to_all(outgoing.reshape(columns * piece_rows, block_width), 'fsdp...  25.4 us
    all_to_all x1, blocking collectives, turns_attach(): lax.all_to_all(jnp.stack(jnp.split(w_in, lax.psum(1, device_axis), axis=1...  22.6 us
    all_to_all x1, starting transfers between devices, per_device(): lax.all_to_all(outgoing.reshape(columns * piece_rows, block_width), 'fsdp...  7.28 us
    dot_general x1, matrix products, per_device(): jnp.einsum('kab,kbc->kac', left_product, right_factor, preferred_element_...  3.87 us
  transfers between devices with their start and end apart: 1, of which 1 were waited for; matrix products, arithmetic and copies ran while one was open for 0% of the time, Pallas kernels for 0%

profile of v1, /device:TPU:0, one launch (start us, length us, event | category | flops | bytes accessed | tf_op | source)
XLA Modules:
  0.0 128.8 jit_solution(16596608995751139249)
XLA Ops:
  0.0 0.0 copy-start
  0.0 0.8 reshape.100
  0.9 1.6 %convolution_convert_fusion.3 = bf16[8,128,512]{2,0,1:T(8,128)(2,1)S(1)} fusion(bf16[3,128,512]{2,1,0:T(8,128)(2,1)} %param.4, s32[3]{0:T(128)S(1)} %dynamic-slice_bitcast_fusion), kind=kOutput, calls=%fused_computation.7 | convolution fusion | flops 3670040 | bytes 1441804 | tf_op jit(solution)/shard_map/cj,jrd->crd/dot_general | solution.py:22
  2.5 1.3 %copy.34 = bf16[8,128,512]{2,1,0:T(8,128)(2,1)} copy(bf16[8,128,512]{2,0,1:T(8,128)(2,1)S(1)} %convolution_convert_fusion.3) | data formatting | bytes 2097152 | tf_op jit(solution)/shard_map/convert_element_type | solution.py:24
  3.8 7.3 %all-to-all-start = ((bf16[8,128,512]{2,1,0:T(8,128)(2,1)}), bf16[8,128,512]{2,1,0:T(8,128)(2,1)S(1)}, u32[]{:S(2)}, u32[]{:S(2)}) async-start(bf16[8,128,512]{2,1,0:T(8,128)(2,1)} %copy.34), calls=%async_computation | async-start | bytes 2097152 | tf_op jit(solution)/shard_map/all_to_all | solution.py:25
  11.1 0.1 convert_reduce_fusion.1
  11.2 0.2 convert_reduce_fusion
  11.4 25.4 %all-to-all-done = bf16[8,128,512]{2,1,0:T(8,128)(2,1)S(1)} async-done(((bf16[8,128,512]{2,1,0:T(8,128)(2,1)}), bf16[8,128,512]{2,1,0:T(8,128)(2,1)S(1)}, u32[]{:S(2)}, u32[]{:S(2)}) %all-to-all-start) | async-done | bytes 1048608 | tf_op jit(solution)/shard_map/all_to_all | solution.py:25
  36.8 1.0 fusion.1
  37.9 0.3 copy.36
  38.2 0.1 slice_bitcast_fusion.3
  38.3 0.2 pad_maximum_fusion
  38.5 22.6 %all_to_all.22 = bf16[4,3,128,512]{3,2,1,0:T(8,128)(2,1)S(1)} all-to-all(bf16[4,3,128,512]{3,2,1,0:T(8,128)(2,1)S(1)} %pad_maximum_fusion), channel_id=1, replica_groups=mesh['fsdp'=8,'grp'=4] {'grp'}, dimensions={0} | all-to-all | bytes 3145728 | tf_op jit(solution)/shard_map/all_to_all | solution.py:54
  61.2 1.3 copy.37
  62.4 0.0 copy-done
  62.4 3.9 %convolution_convert_fusion = bf16[3,512,512]{2,1,0:T(8,128)(2,1)S(1)} fusion(bf16[3,512,512]{2,1,0:T(8,128)(2,1)S(1)} %copy-done, bf16[3,512,512]{2,1,0:T(8,128)(2,1)} %bitcast.36, bf16[3,512,512]{2,1,0:T(8,128)(2,1)} %param.5), kind=kOutput, calls=%fused_computation.1 | convolution fusion | flops 1612185600 | bytes 6291456 | tf_op jit(solution)/shard_map/kab,kbc->kac/dot_general | solution.py:68
  66.3 1.4 %copy.40 = bf16[3,512,512]{2,0,1:T(4,128)(2,1)S(1)} copy(bf16[3,512,512]{2,1,0:T(8,128)(2,1)S(1)} %convolution_convert_fusion) | data formatting | bytes 3145728 | tf_op jit(solution)/shard_map/convert_element_type | solution.py:70
  67.7 28.1 %all_to_all.23 = bf16[3,512,512]{2,0,1:T(4,128)(2,1)S(1)} all-to-all(bf16[3,512,512]{2,0,1:T(4,128)(2,1)S(1)} %copy.40), channel_id=1, replica_groups=mesh['fsdp'=8,'grp'=4] {'grp'}, dimensions={1} | all-to-all | bytes 3145728 | tf_op jit(solution)/shard_map/all_to_all | solution.py:71
  95.8 2.2 %bitcast_convert_fusion = bf16[8,128,512]{2,0,1:T(8,128)(2,1)S(1)} fusion(bf16[3,4,128,512]{3,0,2,1:T(4,128)(2,1)S(1)} %bitcast.35, pred[3,8]{1,0:T(4,128)(4,1)S(1)} %iota_compare_fusion.1, pred[4,8]{1,0:T(4,128)(4,1)S(1)} %fusion.19), kind=kOutput, calls=%fused_computation | convolution fusion | flops 13107296 | bytes 2621496 | tf_op jit(solution)/shard_map/oks,kord->srd/dot_general | solution.py:73
  98.0 0.3 copy.43
  98.4 28.8 %all_to_all.24 = bf16[8,128,512]{2,1,0:T(8,128)(2,1)S(1)} all-to-all(bf16[8,128,512]{2,1,0:T(8,128)(2,1)S(1)} %copy.43), channel_id=1, replica_groups=mesh['fsdp'=8,'grp'=4] {'fsdp'}, dimensions={0} | all-to-all | bytes 2097152 | tf_op jit(solution)/shard_map/all_to_all | solution.py:76
  127.2 0.8 convolution_convert_fusion.4
  128.0 0.8 copy.45
  (5 shorter events, 0.0 us)
Async XLA Ops:
  0.0 62.4 %copy-start = (bf16[3,512,512]{2,1,0:T(8,128)(2,1)S(1)}, bf16[3,512,512]{2,1,0:T(8,128)(2,1)}, u32[]{:S(2)}) copy-start(bf16[3,512,512]{2,1,0:T(8,128)(2,1)} %param.6) | copy-start | bytes 4718596
  3.8 33.0 %all-to-all-start = ((bf16[8,128,512]{2,1,0:T(8,128)(2,1)}), bf16[8,128,512]{2,1,0:T(8,128)(2,1)S(1)}, u32[]{:S(2)}, u32[]{:S(2)}) async-start(bf16[8,128,512]{2,1,0:T(8,128)(2,1)} %copy.34), calls=%async_computation | async-start | bytes 2097152 | tf_op jit(solution)/shard_map/all_to_all | solution.py:25
